TPU v7x, 256 devices: a whole 4x4x8 slice. The times are simulated.
256 devices in a mesh: fsdp: 64 (over z, x, core), tp: 4 (over y).
Axes of the slice: x: 4, y: 4, z: 8, core: 2. Of those that a mesh axis runs over, the one named last changes fastest.
Arguments:
- master: float32 [2048, 8192], P('fsdp', 'tp'), may hold values from -0.0625 to 0.0625
- first_moment: float32 [2048, 8192], P('fsdp', 'tp'), may hold values from -0.0029296875 to 0.0029296875
- second_moment: float32 [2048, 8192], P('fsdp', 'tp'), may hold values from 2.9802322e-08 to 1.1920929e-06
- gradients: float32 [2048, 8192], P('fsdp', 'tp'), as said below
- step_count: int32 [1], replicated, may hold values from 1 to 8
- tile_round: int32 [256], replicated, may hold values from 0 to 3, as said below
Outputs:
- new_master: float32 [2048, 8192], P('fsdp', 'tp')
- new_first: float32 [2048, 8192], P('fsdp', 'tp')
- new_second: float32 [2048, 8192], P('fsdp', 'tp')
- weights: bfloat16 [2048, 8192], P(None, 'tp')
Inputs may be any that keep to these rules, and one draw needn't show every extreme that they name: `tile_round`: each aligned block of 4 entries (the tiles of one index of fsdp) holds every round number 0 to 3 exactly once. `gradients`: exactly one entry has magnitude 1000 or more; every other entry has magnitude under 100, and in every round without that entry the sum of squares is under 1e5.
All inputs are finite; a program needn't handle non-finite values.
Results may differ from a plain program's by a relative error of at most 0.001.
Values may be sent and summed in bfloat16 or wider, within the bound.
No kernel may reach another device: no remote copies, remote signals or barrier semaphores. Data moves between devices by JAX's collectives and lax.ppermute only.
A program may use at most 64 MiB of HBM per device.

v0:
```python
import functools

import jax
import jax.numpy as jnp
from jax import lax
from jax.sharding import Mesh
from jax.sharding import PartitionSpec as P

ROUNDS = 4
FSDP = ("fsdp_0", "fsdp_1", "fsdp_2")
FSDP_TP = ("fsdp_0", "fsdp_1", "fsdp_2", "tp")


beta_one = 0.9
beta_two = 0.95
adam_epsilon = 1e-08
learning_rate = 0.01
weight_decay = 0.1
clip_norm = 1.0
square_limit = 1000000.0


def one_axis_at_a_time(value, axes):
    return functools.reduce(lax.psum, axes, value)


def local(master, first_moment, second_moment, gradients, step_count, tile_round):
    row_count, columns = master.shape
    tile_rows = row_count // ROUNDS
    shaped = (ROUNDS, tile_rows, columns)
    params = master.reshape(shaped)
    moment_one = first_moment.reshape(shaped)
    moment_two = second_moment.reshape(shaped)
    grads = gradients.reshape(shaped)
    mine = lax.dynamic_slice_in_dim(tile_round, lax.axis_index(FSDP) * ROUNDS, ROUNDS)
    slot_ids = jnp.arange(ROUNDS, dtype=jnp.int32)
    places = [jnp.sum(jnp.where(mine == round_index, slot_ids, 0)) for round_index in range(ROUNDS)]
    grad_tiles = [
        lax.dynamic_index_in_dim(grads, places[round_index], 0, keepdims=False)
        for round_index in range(ROUNDS)
    ]
    squares = [jnp.sum(piece * piece) for piece in grad_tiles]
    totals = one_axis_at_a_time(jnp.stack(squares), FSDP_TP)
    total_list = [totals[round_index] for round_index in range(ROUNDS)]
    broken_list = [totals[round_index] >= square_limit for round_index in range(ROUNDS)]
    steps = step_count[0].astype(jnp.float32)
    correct_one = 1.0 - jnp.power(jnp.float32(beta_one), steps)
    correct_two = 1.0 - jnp.power(jnp.float32(beta_two), steps)
    out_p, out_m, out_v = (params, moment_one, moment_two)
    for round_index in range(ROUNDS):
        where_at = places[round_index]
        old_p = lax.dynamic_index_in_dim(params, where_at, 0, keepdims=False)
        old_m = lax.dynamic_index_in_dim(moment_one, where_at, 0, keepdims=False)
        old_v = lax.dynamic_index_in_dim(moment_two, where_at, 0, keepdims=False)
        scale = jnp.minimum(
            jnp.float32(1.0), clip_norm / (jnp.sqrt(total_list[round_index]) + 1e-06)
        )
        clipped = grad_tiles[round_index] * scale
        moment_new = beta_one * old_m + (1.0 - beta_one) * clipped
        second_new = beta_two * old_v + (1.0 - beta_two) * clipped * clipped
        ratio = moment_new / correct_one / (jnp.sqrt(second_new / correct_two) + adam_epsilon)
        param_new = old_p - learning_rate * (ratio + weight_decay * old_p)
        keeping = broken_list[round_index]
        param_new = jnp.where(keeping, old_p, param_new)
        moment_new = jnp.where(keeping, old_m, moment_new)
        second_new = jnp.where(keeping, old_v, second_new)
        out_p = lax.dynamic_update_index_in_dim(out_p, param_new, where_at, 0)
        out_m = lax.dynamic_update_index_in_dim(out_m, moment_new, where_at, 0)
        out_v = lax.dynamic_update_index_in_dim(out_v, second_new, where_at, 0)
    new_master = out_p.reshape(row_count, columns)
    weights = lax.all_gather(new_master.astype(jnp.bfloat16), FSDP, axis=0, tiled=True)
    return (
        new_master,
        out_m.reshape(row_count, columns),
        out_v.reshape(row_count, columns),
        weights,
    )


def solution(mesh):
    finer = Mesh(
        mesh.devices.reshape(8, 4, 2, mesh.shape["tp"]), ("fsdp_0", "fsdp_1", "fsdp_2", "tp")
    )
    return jax.shard_map(
        local,
        mesh=finer,
        in_specs=(P(FSDP, "tp"), P(FSDP, "tp"), P(FSDP, "tp"), P(FSDP, "tp"), P(), P()),
        out_specs=(P(FSDP, "tp"), P(FSDP, "tp"), P(FSDP, "tp"), P(None, "tp")),
        check_vma=False,
    )
```

profile of v0, /device:TPU:1, one launch (start us, length us, event | category | flops | bytes accessed | tf_op | source)
XLA Modules:
  0.0 175.0 jit_solution(18027234400804235524)
XLA Ops:
  7.2 0.0 all-gather.2.cloned.1.call-start
  7.2 1.4 fusion.9
  16.4 1.6 multiply_reduce_fusion.3
  18.0 2.7 %pad_maximum_fusion = f32[4]{0:T(128)S(1)} fusion(f32[1]{0:T(128)} %bitcast.5, f32[1]{0:T(128)} %bitcast.4, f32[1]{0:T(128)} %bitcast.3, f32[1]{0:T(128)} %bitcast.2), kind=kLoop, calls=%fused_computation.40 | loop fusion | flops 12 | bytes 32 | tf_op jit(solution)/shard_map/stack | solution.py:43
  20.7 17.3 %psum.28 = f32[4]{0:T(128)S(1)} all-reduce(f32[4]{0:T(128)S(1)} %pad_maximum_fusion), channel_id=1, replica_groups=mesh['fsdp_0'=8,'fsdp_1'=4,'fsdp_2'=2,'tp'=4] {'fsdp_0'}, use_global_device_ids=true, to_apply=%region_8.9 | all-reduce | flops 4 | bytes 32 | tf_op jit(solution)/shard_map/psum | solution.py:24
  37.9 8.5 %psum.29 = f32[4]{0:T(128)S(1)} all-reduce(f32[4]{0:T(128)S(1)} %psum.28), channel_id=1, replica_groups=mesh['fsdp_0'=8,'fsdp_1'=4,'fsdp_2'=2,'tp'=4] {'fsdp_1'}, use_global_device_ids=true, to_apply=%region_9.10 | all-reduce | flops 4 | bytes 32 | tf_op jit(solution)/shard_map/psum | solution.py:24
  46.4 8.3 %psum.30 = f32[4]{0:T(128)S(1)} all-reduce(f32[4]{0:T(128)S(1)} %psum.29), channel_id=1, replica_groups=mesh['fsdp_0'=8,'fsdp_1'=4,'fsdp_2'=2,'tp'=4] {'fsdp_2'}, use_global_device_ids=true, to_apply=%region_10.11 | all-reduce | flops 4 | bytes 32 | tf_op jit(solution)/shard_map/psum | solution.py:24
  54.7 8.7 %psum.31 = f32[4]{0:T(128)S(1)} all-reduce(f32[4]{0:T(128)S(1)} %psum.30), channel_id=1, replica_groups=mesh['fsdp_0'=8,'fsdp_1'=4,'fsdp_2'=2,'tp'=4] {'tp'}, use_global_device_ids=true, to_apply=%region_11.12 | all-reduce | flops 4 | bytes 32 | tf_op jit(solution)/shard_map/psum | solution.py:24
  63.4 0.6 fusion.12
  70.3 1.0 copy.12
  71.2 0.9 copy.17
  72.2 0.9 copy.10
  73.1 0.9 select_dynamic-update-slice_fusion.3
  74.0 1.1 select_dynamic-update-slice_fusion.2
  75.0 1.1 select_dynamic-update-slice_fusion.1
  76.1 1.1 select_dynamic-update-slice_fusion
  77.2 1.0 select_dynamic-update-slice_fusion.6
  78.2 0.9 select_dynamic-update-slice_fusion.5
  79.1 1.0 select_dynamic-update-slice_fusion.4
  80.1 0.0 copy-start
  80.2 0.7 bitcast_convert_fusion
  80.9 0.0 all-gather.2.cloned.1.call-update
  80.9 78.8 %all-gather.2.cloned.1.call-done = bf16[2048,2048]{1,0:T(8,128)(2,1)} async-done(((bf16[32,2048]{1,0:T(8,128)(2,1)}), bf16[2048,2048]{1,0:T(8,128)(2,1)}) %all-gather.2.cloned.1.call-update) | async-done | bytes 8388624 | tf_op jit(solution)/shard_map/all_gather | solution.py:71
  159.7 8.4 %copy.24 = bf16[2048,2048]{1,0:T(8,128)(2,1)} copy(bf16[2048,2048]{1,0:T(8,128)(2,1)} %all-gather.2.cloned.1.call-done) | data formatting | bytes 16777216
  (5 shorter events, 0.0 us)
Async XLA Ops:
  7.2 152.6 %all-gather.2.cloned.1.call-start = ((), (), s32[]{:S(2)}) async-start(), calls=%async_computation | async-start | bytes 8519680 | tf_op jit(solution)/shard_map/all_gather | solution.py:71
  77.2 90.9 %copy-start.2 = (f32[4,8,2048]{2,1,0:T(8,128)}, f32[4,8,2048]{2,1,0:T(8,128)S(1)}, u32[]{:S(2)}) copy-start(f32[4,8,2048]{2,1,0:T(8,128)S(1)} %get-tuple-element.12) | copy-start | bytes 786436
  80.1 88.0 %copy-start = (f32[4,8,2048]{2,1,0:T(8,128)}, f32[4,8,2048]{2,1,0:T(8,128)S(1)}, u32[]{:S(2)}) copy-start(f32[4,8,2048]{2,1,0:T(8,128)S(1)} %get-tuple-element.20) | copy-start | bytes 786436
  80.1 88.0 %copy-start.1 = (f32[4,8,2048]{2,1,0:T(8,128)}, f32[4,8,2048]{2,1,0:T(8,128)S(1)}, u32[]{:S(2)}) copy-start(f32[4,8,2048]{2,1,0:T(8,128)S(1)} %get-tuple-element.19) | copy-start | bytes 786436
Sparse Core Ops, SparseCore 0:
  81.0 78.6 all-gather.1
where the time goes:
time: 176 us; the launch traced here: 175 us
  waiting for transfers between devices  78.8 us (45%)
  blocking collectives  42.8 us (24%)
  between operations  28.1 us (16%)
  other arithmetic  13.4 us (8%)
  local copies, waits for them, and re-layouts  11.9 us (7%)
    all_gather x1, waiting for transfers between devices, local(): lax.all_gather(new_master.astype(jnp.bfloat16), FSDP, axis=0, tiled=True)  78.8 us
    psum x4, blocking collectives, one_axis_at_a_time(): return functools.reduce(lax.psum, axes, value)  42.8 us
    unnamed x10, local copies, waits for them, and re-layouts  11.3 us
    dynamic_update_slice x4, other arithmetic, local(): out_v = lax.dynamic_update_index_in_dim(out_v, second_new, where_at, 0)  4.11 us
  transfers between devices with their start and end apart: 1, of which 1 were waited for; matrix products, arithmetic and copies ran while one was open for 0% of the time, Pallas kernels for 0%

commit v1 on v0

v1 whole, which is shorter than its diff:
```python
import jax
import jax.numpy as jnp
from jax import lax
from jax.sharding import Mesh
from jax.sharding import PartitionSpec as P

ROUNDS = 4
FSDP = ("z", "x", "core")
ALL = ("z", "x", "core", "tp")


beta_one = 0.9
beta_two = 0.95
adam_epsilon = 1e-08
learning_rate = 0.01
weight_decay = 0.1
clip_norm = 1.0
square_limit = 1000000.0


def sum_over_devices(value, devices):
    copies = jnp.broadcast_to(value, (devices,) + value.shape)
    return jnp.sum(lax.all_to_all(copies, ALL, 0, 0, tiled=True), axis=0)


def local(devices, master, first_moment, second_moment, gradients, step_count, tile_round):
    row_count, columns = master.shape
    shaped = (ROUNDS, row_count // ROUNDS, columns)
    params = master.reshape(shaped)
    moment_one = first_moment.reshape(shaped)
    moment_two = second_moment.reshape(shaped)
    grads = gradients.reshape(shaped)
    mine = lax.dynamic_slice_in_dim(tile_round, lax.axis_index(FSDP) * ROUNDS, ROUNDS)
    is_round = mine[None, :] == jnp.arange(ROUNDS, dtype=jnp.int32)[:, None]
    squares = jnp.sum(grads * grads, axis=(1, 2))
    totals = sum_over_devices(
        jnp.sum(jnp.where(is_round, squares[None, :], 0.0), axis=1), devices
    )
    total_of_slot = jnp.sum(jnp.where(is_round, totals[:, None], 0.0), axis=0)
    total_of_slot = total_of_slot.reshape(ROUNDS, 1, 1)
    scale = jnp.minimum(jnp.float32(1.0), clip_norm / (jnp.sqrt(total_of_slot) + 1e-06))
    keeping = total_of_slot >= square_limit
    steps = step_count[0].astype(jnp.float32)
    correct_one = 1.0 - jnp.power(jnp.float32(beta_one), steps)
    correct_two = 1.0 - jnp.power(jnp.float32(beta_two), steps)
    clipped = grads * scale
    moment_new = beta_one * moment_one + (1.0 - beta_one) * clipped
    second_new = beta_two * moment_two + (1.0 - beta_two) * clipped * clipped
    ratio = moment_new / correct_one / (jnp.sqrt(second_new / correct_two) + adam_epsilon)
    param_new = params - learning_rate * (ratio + weight_decay * params)
    out_p = jnp.where(keeping, params, param_new).reshape(row_count, columns)
    out_m = jnp.where(keeping, moment_one, moment_new).reshape(row_count, columns)
    out_v = jnp.where(keeping, moment_two, second_new).reshape(row_count, columns)
    weights = lax.all_gather(out_p.astype(jnp.bfloat16), FSDP, axis=0, tiled=True)
    return out_p, out_m, out_v, weights


def solution(mesh):
    tp = mesh.shape["tp"]
    finer = Mesh(mesh.devices.reshape(8, 4, 2, tp), ALL)
    spec = P(FSDP, "tp")

    def step(*args):
        return local(mesh.devices.size, *args)

    return jax.shard_map(
        step,
        mesh=finer,
        in_specs=(spec, spec, spec, spec, P(), P()),
        out_specs=(spec, spec, spec, P(None, "tp")),
        check_vma=False,
    )
```

time: 176 us -> 134 us (0.76)
  blocking collectives: 42.8 us -> 0 us
  starting transfers between devices: 0.04 us -> 15.7 us
  between operations: 28.1 us -> 14.8 us
  waiting for transfers between devices: 78.8 us -> 89 us
  other arithmetic: 13.4 us -> 4.15 us
    psum x4 -> x0, blocking collectives: 42.8 us -> none  [one_axis_at_a_time(): return functools.reduce(lax.psum, axes, value)]
    all_to_all x0 -> x1, starting transfers between devices: none -> 15.6 us  [sum_over_devices(): return jnp.sum(lax.all_to_all(copies, ALL, 0, 0, tiled=True), axis=0)]
    all_to_all x0 -> x1, waiting for transfers between devices: none -> 11.9 us  [sum_over_devices(): return jnp.sum(lax.all_to_all(copies, ALL, 0, 0, tiled=True), axis=0)]
    dynamic_update_slice x7 -> x0, other arithmetic: 7 us -> none  [the longest x4 4.11 us: local(): out_v = lax.dynamic_update_index_in_dim(out_v, second_new, where_at, 0)]
    unnamed x10 -> x1, local copies, waits for them, and re-layouts: 11.3 us -> 8.44 us
    another operation x1 -> x0, other arithmetic: 2.66 us -> none  [local(): totals = one_axis_at_a_time(jnp.stack(squares), FSDP_TP)]
  transfers between devices with their start and end apart: 1 -> 2, of which waited for: 1 -> 2; matrix products, arithmetic and copies ran while one was open for 0% -> 0% of each run, Pallas kernels for 0% -> 0%
where the time goes in v1:
time: 134 us
  waiting for transfers between devices  89 us (66%)
  starting transfers between devices  15.7 us (12%)
  between operations  14.8 us (11%)
  local copies, waits for them, and re-layouts  10.3 us (8%)
  other arithmetic  4.15 us (3%)
    all_gather x1, waiting for transfers between devices, local(): lax.all_gather(out_p.astype(jnp.bfloat16), FSDP, axis=0, tiled=True)  77.1 us
    all_to_all x1, starting transfers between devices, sum_over_devices(): return jnp.sum(lax.all_to_all(copies, ALL, 0, 0, tiled=True), axis=0)  15.6 us
    all_to_all x1, waiting for transfers between devices, sum_over_devices(): return jnp.sum(lax.all_to_all(copies, ALL, 0, 0, tiled=True), axis=0)  11.9 us
    unnamed x1, local copies, waits for them, and re-layouts  8.44 us
  transfers between devices with their start and end apart: 2, of which 2 were waited for; matrix products, arithmetic and copies ran while one was open for 0% of the time, Pallas kernels for 0%

profile of v1, /device:TPU:1, one launch (start us, length us, event | category | flops | bytes accessed | tf_op | source)
XLA Modules:
  0.0 133.9 jit_solution(13358930770020262899)
XLA Ops:
  7.2 1.1 multiply_reduce_fusion
  8.2 0.1 reduce_sum.44
  8.3 0.8 dynamic_slice.3
  9.1 0.1 reduce_sum.45
  9.2 0.1 select_reduce_fusion.1
  9.3 0.7 broadcast_in_dim.49
  10.1 15.6 %all-to-all-start = ((f32[256,1,4]{2,1,0:T(1,128)}), f32[256,1,4]{2,1,0:T(1,128)S(1)}, u32[]{:S(2)}, u32[]{:S(2)}) async-start(f32[256,1,4]{2,1,0:T(1,128)} %broadcast_in_dim.49), calls=%async_computation | async-start | bytes 262144 | tf_op jit(solution)/shard_map/all_to_all | solution.py:23
  25.7 0.0 all-gather.2.cloned.1.call-start
  26.5 11.9 %all-to-all-done = f32[256,1,4]{2,1,0:T(1,128)S(1)} async-done(((f32[256,1,4]{2,1,0:T(1,128)}), f32[256,1,4]{2,1,0:T(1,128)S(1)}, u32[]{:S(2)}, u32[]{:S(2)}) %all-to-all-start) | async-done | bytes 4128 | tf_op jit(solution)/shard_map/all_to_all | solution.py:23
  38.4 0.3 reduce_sum.47
  38.7 0.1 select_reduce_fusion
  38.8 0.1 broadcast_in_dim.51
  38.9 0.1 broadcast_in_dim.52
  38.9 0.1 mul.79
  39.0 0.1 mul.80
  39.1 2.4 %fusion.3 = (bf16[32,2048]{1,0:T(8,128)(2,1)}, f32[32,2048]{1,0:T(8,128)}, f32[32,2048]{1,0:T(8,128)}, f32[32,2048]{1,0:T(8,128)}) fusion(f32[32,2048]{1,0:T(8,128)} %param.6, f32[]{:T(128)} %bitcast.1, f32[32,2048]{1,0:T(8,128)} %param.8, f32[]{:T(128)} %bitcast, f32[32,2048]{1,0:T(8,128)} %param.9, f32[32]{0:T(128)S(1)} %mul.80, f32[32,2048]{1,0:T(8,128)} %param.7, ...), kind=kLoop, calls=%fused_computation.12 | loop fusion | flops 1310720 | bytes 1966248 | tf_op jit(solution)/shard_map/convert_element_type | solution.py:54
  41.5 0.0 all-gather.2.cloned.1.call-update
  41.6 77.1 %all-gather.2.cloned.1.call-done = bf16[2048,2048]{1,0:T(8,128)(2,1)} async-done(((bf16[32,2048]{1,0:T(8,128)(2,1)}), bf16[2048,2048]{1,0:T(8,128)(2,1)}) %all-gather.2.cloned.1.call-update) | async-done | bytes 8388624 | tf_op jit(solution)/shard_map/all_gather | solution.py:54
  118.6 8.4 %copy.14 = bf16[2048,2048]{1,0:T(8,128)(2,1)} copy(bf16[2048,2048]{1,0:T(8,128)(2,1)} %all-gather.2.cloned.1.call-done) | data formatting | bytes 16777216
  (2 shorter events, 0.0 us)
Async XLA Ops:
  10.1 28.3 %all-to-all-start = ((f32[256,1,4]{2,1,0:T(1,128)}), f32[256,1,4]{2,1,0:T(1,128)S(1)}, u32[]{:S(2)}, u32[]{:S(2)}) async-start(f32[256,1,4]{2,1,0:T(1,128)} %broadcast_in_dim.49), calls=%async_computation | async-start | bytes 262144 | tf_op jit(solution)/shard_map/all_to_all | solution.py:23
  25.7 92.9 %all-gather.2.cloned.1.call-start = ((), (), s32[]{:S(2)}) async-start(), calls=%async_computation.1 | async-start | bytes 8519680 | tf_op jit(solution)/shard_map/all_gather | solution.py:54
Sparse Core Ops, SparseCore 0:
  41.7 76.8 all-gather.1
